TPU v7x, 32 devices: a whole 2x2x4 slice. The times are simulated.
32 devices in a mesh: head: 2 (over y), outer: 4 (over z), inner: 4 (over x, core).
Axes of the slice: x: 2, y: 2, z: 4, core: 2. Of those that a mesh axis runs over, the one named last changes fastest.
Arguments:
- queries: bfloat16 [1024, 2048], P('outer', ('head', 'inner')), may hold values from -100 to 100
- keys: bfloat16 [1024, 256], P('outer', 'head'), may hold values from -5 to 5
- values: bfloat16 [1024, 256], P('outer', 'head'), may hold values from -6 to 6
- grad_out: bfloat16 [1024, 2048], P('outer', ('head', 'inner')), may hold values from -24 to 24
- hidden_in: bfloat16 [1024, 8192], P('outer', ('head', 'inner')), may hold values from -6 to 6
- adapter_a: bfloat16 [8192, 16], P(('head', 'inner')), may hold values from -0.0625 to 0.0625
- adapter_b: bfloat16 [16, 256], P(None, 'head'), may hold values from -1.5 to 1.5
- block_order: int32 [8], replicated, may hold values from 0 to 7, each once
- doc_ids: int32 [1024], replicated, may hold values from 0 to 3, never falling along the last dimension, each value on 1 to 512 neighbouring positions
Outputs:
- grad_query: bfloat16 [1024, 2048], P('outer', ('head', 'inner'))
- grad_key: bfloat16 [1024, 256], P('outer', 'head')
- grad_value: bfloat16 [1024, 256], P('outer', 'head')
- grad_a: float32 [8192, 16], P(('head', 'inner'))
- grad_b: float32 [16, 256], P(None, 'head')
Inputs may be any that keep to these rules, and one draw needn't show every extreme that they name: `block_order`: a permutation of the stored blocks. `doc_ids`: never falling along positions; each document has 1 to 512 positions.
All inputs are finite; a program needn't handle non-finite values.
Results may differ from a plain program's by a relative error of at most 0.024.
Values may be sent and summed in bfloat16 or wider, within the bound.
A program may use at most 64 MiB of HBM per device.

v0:
```python
import jax
import jax.numpy as jnp
from jax import lax
from jax.sharding import PartitionSpec as P

HEAD_DIM = 128
NEGATIVE = -1e30


def passed_along(value, axis, steps):
    count = lax.axis_size(axis)
    pairs = [(source, (source + steps) % count) for source in range(count)]
    return lax.ppermute(value, axis, pairs)


def block_meta(block_table, doc_table, block_id, half_rows):
    first_pos = block_table[block_id] * half_rows
    places = first_pos + jnp.arange(half_rows, dtype=jnp.int32)
    owners = lax.dynamic_slice_in_dim(doc_table, first_pos, half_rows, 0)
    return (places, owners)


def joined_meta(first, second):
    return (jnp.concatenate((first[0], second[0]), 0), jnp.concatenate((first[1], second[1]), 0))


def visible(query_meta, key_meta):
    return (key_meta[0][None, :] <= query_meta[0][:, None]) & (
        key_meta[1][None, :] == query_meta[1][:, None]
    )


def tile_scores(query_tile, key_rows, scaling):
    return (
        jnp.einsum("tkgd,skd->kgts", query_tile, key_rows, preferred_element_type=jnp.float32)
        * scaling
    )


def forward_tile(carried, masked, query_tile, key_tile, value_tile, scaling):
    peak_score, totals, summed = carried
    kv_local = query_tile.shape[1]
    key_rows = key_tile.reshape(key_tile.shape[0], kv_local, -1)
    value_rows = value_tile.reshape(value_tile.shape[0], kv_local, -1)
    scores = jnp.where(masked, tile_scores(query_tile, key_rows, scaling), NEGATIVE)
    new_peak = jnp.maximum(peak_score, jnp.max(scores, axis=-1))
    weights = jnp.where(masked, jnp.exp(scores - new_peak[..., None]), 0.0)
    factor = jnp.exp(peak_score - new_peak)
    summed = summed * factor[..., None] + jnp.einsum(
        "kgts,skd->kgtd",
        weights.astype(jnp.bfloat16),
        value_rows,
        preferred_element_type=jnp.float32,
    )
    return (new_peak, totals * factor + jnp.sum(weights, axis=-1), summed)


def backward_tile(
    carried, masked, query_tile, grad_tile, lse_tile, delta_tile, key_tile, value_tile, scaling
):
    grad_query, grad_key, grad_value = carried
    kv_local = query_tile.shape[1]
    key_rows = key_tile.reshape(key_tile.shape[0], kv_local, -1)
    value_rows = value_tile.reshape(value_tile.shape[0], kv_local, -1)
    scores = tile_scores(query_tile, key_rows, scaling)
    prob_tile = jnp.where(masked, jnp.exp(scores - lse_tile[..., None]), 0.0)
    grad_value = grad_value + jnp.einsum(
        "kgts,tkgd->skd",
        prob_tile.astype(jnp.bfloat16),
        grad_tile,
        preferred_element_type=jnp.float32,
    )
    dot_tile = jnp.einsum(
        "tkgd,skd->kgts", grad_tile, value_rows, preferred_element_type=jnp.float32
    )
    slopes = (prob_tile * (dot_tile - delta_tile[..., None])).astype(jnp.bfloat16)
    grad_query = grad_query + jnp.einsum(
        "kgts,skd->tkgd", slopes, key_rows, preferred_element_type=jnp.float32
    )
    grad_key = grad_key + jnp.einsum(
        "kgts,tkgd->skd", slopes, query_tile, preferred_element_type=jnp.float32
    )
    return (grad_query, grad_key, grad_value)


def anchors(member, cycle_size, counter):
    return ((member - counter) % cycle_size, (member - counter) % cycle_size)


def advance(current):
    return tuple(passed_along((current[0], current[1], current[2], current[3]), "outer", 1))


def rotate_grads(key_acc, value_acc):
    moved = (
        passed_along(key_acc.astype(jnp.bfloat16), "outer", 1).astype(key_acc.dtype),
        passed_along(value_acc.astype(jnp.bfloat16), "outer", 1).astype(value_acc.dtype),
    )
    return (moved[0], moved[1])


def on_device(
    queries, keys, values, grad_out, hidden_in, adapter_a, adapter_b, block_order, doc_ids
):
    cycle_size = lax.axis_size("outer")
    member = lax.axis_index("outer")
    tokens = queries.shape[0]
    half_rows = tokens // 2
    kv_local = keys.shape[1] // HEAD_DIM
    grp_local = queries.shape[1] // (kv_local * HEAD_DIM)
    scaling = HEAD_DIM ** (-0.5)
    query_rows = queries.reshape(tokens, kv_local, grp_local, HEAD_DIM)
    grad_rows = grad_out.reshape(tokens, kv_local, grp_local, HEAD_DIM)
    own_meta = joined_meta(
        block_meta(block_order, doc_ids, 2 * member, half_rows),
        block_meta(block_order, doc_ids, 2 * member + 1, half_rows),
    )
    local_keys = (keys[:half_rows], values[:half_rows], keys[half_rows:], values[half_rows:])
    low_partial = jnp.dot(hidden_in, adapter_a, preferred_element_type=jnp.float32)
    low_rank = lax.psum(low_partial, ("head", "inner")).astype(jnp.bfloat16)

    def sweep(counter, current, handle, carried):
        upper_src, lower_src = anchors(member, cycle_size, counter)
        key_meta = joined_meta(
            block_meta(block_order, doc_ids, 2 * upper_src, half_rows),
            block_meta(block_order, doc_ids, 2 * lower_src + 1, half_rows),
        )
        masked = visible(own_meta, key_meta)
        key_tile = jnp.concatenate((current[0], current[2]), 0)
        value_tile = jnp.concatenate((current[1], current[3]), 0)

        def active(present):
            return handle(present, masked, key_tile, value_tile)

        def resting(present):
            return present

        return lax.cond(jnp.any(masked), active, resting, carried)

    def forward_handle(present, masked, key_tile, value_tile):
        return forward_tile(present, masked, query_rows, key_tile, value_tile, scaling)

    start_state = (
        jnp.full((kv_local, grp_local, tokens), NEGATIVE, jnp.float32),
        jnp.zeros((kv_local, grp_local, tokens), jnp.float32),
        jnp.zeros((kv_local, grp_local, tokens, HEAD_DIM), jnp.float32),
    )

    def forward_turn(counter, loop_state):
        current, state = loop_state
        state = sweep(counter, current, forward_handle, state)
        return (advance(current), state)

    current, state = lax.fori_loop(0, cycle_size - 1, forward_turn, (local_keys, start_state))
    state = sweep(cycle_size - 1, current, forward_handle, state)
    peak_score, totals, summed = state
    lse_rows = peak_score + jnp.log(totals)
    output = summed / totals[..., None]
    delta_rows = jnp.sum(
        output * jnp.transpose(grad_rows, (1, 2, 0, 3)).astype(jnp.float32), axis=-1
    )
    empty_query = jnp.zeros((tokens, kv_local, grp_local, HEAD_DIM), jnp.float32)

    def backward_handle(present, masked, key_tile, value_tile):
        return backward_tile(
            present,
            masked,
            query_rows,
            grad_rows,
            lse_rows,
            delta_rows,
            key_tile,
            value_tile,
            scaling,
        )

    def backward_turn(counter, loop_state):
        current, carried = loop_state
        grad_query, key_acc, value_acc = sweep(counter, current, backward_handle, carried)
        key_acc, value_acc = rotate_grads(key_acc, value_acc)
        return (advance(current), (grad_query, key_acc, value_acc))

    empty_keys = jnp.zeros((tokens, kv_local, HEAD_DIM), jnp.float32)
    current, carried = lax.fori_loop(
        0, cycle_size - 1, backward_turn, (local_keys, (empty_query, empty_keys, empty_keys))
    )
    grad_queries, key_acc, value_acc = sweep(cycle_size - 1, current, backward_handle, carried)
    key_acc, value_acc = rotate_grads(key_acc, value_acc)
    key_acc, value_acc = (
        lax.psum(key_acc.astype(jnp.bfloat16), "inner").astype(jnp.float32),
        lax.psum(value_acc.astype(jnp.bfloat16), "inner").astype(jnp.float32),
    )
    grad_query = (grad_queries * scaling).astype(jnp.bfloat16).reshape(tokens, -1)
    grad_key = (key_acc * scaling).astype(jnp.bfloat16).reshape(tokens, -1)
    grad_value = value_acc.astype(jnp.bfloat16).reshape(tokens, -1)
    back_partial = lax.dot_general(
        grad_key, adapter_b, (((1,), (1,)), ((), ())), preferred_element_type=jnp.float32
    )
    back_rank = lax.psum(back_partial, "head").astype(jnp.bfloat16)
    grad_a_part = lax.dot_general(
        hidden_in, back_rank, (((0,), (0,)), ((), ())), preferred_element_type=jnp.float32
    )
    grad_b_part = lax.dot_general(
        low_rank, grad_key, (((0,), (0,)), ((), ())), preferred_element_type=jnp.float32
    )
    grad_a, grad_b = lax.psum((grad_a_part, grad_b_part), "outer")
    return (grad_query, grad_key, grad_value, grad_a, grad_b)


def solution(mesh):
    in_specs = (
        P("outer", ("head", "inner")),
        P("outer", "head"),
        P("outer", "head"),
        P("outer", ("head", "inner")),
        P("outer", ("head", "inner")),
        P(("head", "inner"), None),
        P(None, "head"),
        P(),
        P(),
    )
    out_specs = (
        P("outer", ("head", "inner")),
        P("outer", "head"),
        P("outer", "head"),
        P(("head", "inner"), None),
        P(None, "head"),
    )
    return jax.shard_map(
        on_device, mesh=mesh, in_specs=in_specs, out_specs=out_specs, check_vma=False
    )
```

profile of v0, /device:TPU:0, one launch (start us, length us, event | category | flops | bytes accessed | tf_op | source)
XLA Modules:
  0.0 191.0 jit_solution(2732203361276319303)
XLA Ops:
  14.9 30.7 %while.55 = (s32[]{:T(128)}, bf16[128,128]{1,0:T(8,128)(2,1)S(1)}, bf16[128,128]{1,0:T(8,128)(2,1)S(1)}, bf16[128,128]{1,0:T(8,128)(2,1)S(1)}, bf16[128,128]{1,0...) while((s32[]{:T(128)}, bf16[128,128]{1,0:T(8,128)(2,1)S(1)}, ...), condition=%wide.region_7.8_spmd, body=%wide.region_1.7_spmd.sunk | while | flops 68946208 | bytes 3714876 | solution.py:154
  14.9 3.1 %collective-permute-start = (bf16[128,128]{1,0:T(8,128)(2,1)S(1)}, bf16[128,128]{1,0:T(8,128)(2,1)S(1)}, u32[]{:S(2)}, u32[]{:S(2)}) collective-permute-start(bf16[128,128]{1,0:T(8,128)(2,1)S(1)} %copy.63), channel_id=1, source_target_pairs={{0,4},{4,8},{8,12},{12,0},{1,5},{5,9},{9,13},{13,1},{2,6},{6,10},{... | collective-permute-start | bytes 98312 | tf_op jit(solution)/shard_map/while/body/eval_jaxpr/ppermute | solution.py:13
  18.1 1.6 collective-permute-start.1
  19.6 1.6 collective-permute-start.2
  24.7 0.8 conditional.9
  25.6 1.3 collective-permute-done.3
  27.4 1.6 collective-permute-start.1
  29.0 1.6 collective-permute-start.2
  30.6 1.3 collective-permute-start.3
  33.9 0.8 fusion.112
  35.3 0.8 conditional.9
  36.8 1.6 collective-permute-start.1
  38.4 1.6 collective-permute-start.2
  39.9 1.3 collective-permute-start.3
  43.3 0.8 fusion.112
  44.7 0.8 conditional.9
  45.7 0.9 conditional.4
  46.7 50.4 %while.56 = (s32[]{:T(128)}, bf16[128,128]{1,0:T(8,128)(2,1)S(1)}, bf16[128,128]{1,0:T(8,128)(2,1)S(1)}, bf16[128,128]{1,0:T(8,128)(2,1)S(1)}, bf16[128,128]{1,0...) while((s32[]{:T(128)}, bf16[128,128]{1,0:T(8,128)(2,1)S(1)}, ...), condition=%wide.region_17.18_spmd.clone, body=%wide.region_13.0_spmd.clone.sunk | while | flops 169542432 | bytes 7159750 | solution.py:184
  50.3 1.3 conditional.10
  51.7 1.2 collective-permute-start.8
  52.9 1.6 collective-permute-start.4
  54.6 2.1 %collective-permute-start.5 = (bf16[128,128]{1,0:T(8,128)(2,1)S(1)}, bf16[128,128]{1,0:T(8,128)(2,1)S(1)}, u32[]{:S(2)}, u32[]{:S(2)}) collective-permute-start(bf16[128,128]{1,0:T(8,128)(2,1)S(1)} %copy.96), channel_id=1, source_target_pairs={{0,4},{4,8},{8,12},{12,0},{1,5},{5,9},{9,13},{13,1},{2,6},{6,10},{... | collective-permute-start | bytes 98312 | tf_op jit(solution)/shard_map/while/body/eval_jaxpr/ppermute | solution.py:13
  56.8 1.3 collective-permute-done.9
  59.1 1.1 collective-permute-done.5
  60.3 2.1 %collective-permute-done.6 = bf16[128,128]{1,0:T(8,128)(2,1)S(1)} collective-permute-done((bf16[128,128]{1,0:T(8,128)(2,1)S(1)}, bf16[128,128]{1,0:T(8,128)(2,1)S(1)}, u32[]{:S(2)}, u32[]{:S(2)}) %collective-permute-start.6) | collective-permute-done | bytes 32800 | tf_op jit(solution)/shard_map/while/body/eval_jaxpr/ppermute | solution.py:13
  62.4 1.4 collective-permute-done.7
  67.3 1.3 conditional.10
  68.8 1.7 collective-permute-start.4
  70.5 3.2 %collective-permute-start.5 = (bf16[128,128]{1,0:T(8,128)(2,1)S(1)}, bf16[128,128]{1,0:T(8,128)(2,1)S(1)}, u32[]{:S(2)}, u32[]{:S(2)}) collective-permute-start(bf16[128,128]{1,0:T(8,128)(2,1)S(1)} %copy.96), channel_id=1, source_target_pairs={{0,4},{4,8},{8,12},{12,0},{1,5},{5,9},{9,13},{13,1},{2,6},{6,10},{... | collective-permute-start | bytes 98312 | tf_op jit(solution)/shard_map/while/body/eval_jaxpr/ppermute | solution.py:13
  73.8 1.0 collective-permute-done.9
  76.2 3.2 %collective-permute-done.6 = bf16[128,128]{1,0:T(8,128)(2,1)S(1)} collective-permute-done((bf16[128,128]{1,0:T(8,128)(2,1)S(1)}, bf16[128,128]{1,0:T(8,128)(2,1)S(1)}, u32[]{:S(2)}, u32[]{:S(2)}) %collective-permute-start.6) | collective-permute-done | bytes 32800 | tf_op jit(solution)/shard_map/while/body/eval_jaxpr/ppermute | solution.py:13
  79.4 1.0 collective-permute-done.7
  84.0 1.3 conditional.10
  85.5 2.4 %collective-permute-start.4 = (bf16[128,128]{1,0:T(8,128)(2,1)S(1)}, bf16[128,128]{1,0:T(8,128)(2,1)S(1)}, u32[]{:S(2)}, u32[]{:S(2)}) collective-permute-start(bf16[128,128]{1,0:T(8,128)(2,1)S(1)} %copy.95), channel_id=1, source_target_pairs={{0,4},{4,8},{8,12},{12,0},{1,5},{5,9},{9,13},{13,1},{2,6},{6,10},{... | collective-permute-start | bytes 98312 | tf_op jit(solution)/shard_map/while/body/eval_jaxpr/ppermute | solution.py:13
  87.9 2.5 %collective-permute-start.5 = (bf16[128,128]{1,0:T(8,128)(2,1)S(1)}, bf16[128,128]{1,0:T(8,128)(2,1)S(1)}, u32[]{:S(2)}, u32[]{:S(2)}) collective-permute-start(bf16[128,128]{1,0:T(8,128)(2,1)S(1)} %copy.96), channel_id=1, source_target_pairs={{0,4},{4,8},{8,12},{12,0},{1,5},{5,9},{9,13},{13,1},{2,6},{6,10},{... | collective-permute-start | bytes 98312 | tf_op jit(solution)/shard_map/while/body/eval_jaxpr/ppermute | solution.py:13
  90.4 1.0 collective-permute-done.9
  92.6 1.3 collective-permute-done.5
  93.9 2.1 %collective-permute-done.6 = bf16[128,128]{1,0:T(8,128)(2,1)S(1)} collective-permute-done((bf16[128,128]{1,0:T(8,128)(2,1)S(1)}, bf16[128,128]{1,0:T(8,128)(2,1)S(1)}, u32[]{:S(2)}, u32[]{:S(2)}) %collective-permute-start.6) | collective-permute-done | bytes 32800 | tf_op jit(solution)/shard_map/while/body/eval_jaxpr/ppermute | solution.py:13
  96.1 1.0 collective-permute-done.7
  97.2 1.3 conditional.5
  99.5 5.0 %collective-permute-done.11 = bf16[256,1,128]{2,0,1:T(8,128)(2,1)S(1)} collective-permute-done((bf16[256,1,128]{2,0,1:T(8,128)(2,1)S(1)}, bf16[256,1,128]{2,0,1:T(8,128)(2,1)S(1)}, u32[]{:S(2)}, u32[]{:S(2)}) %collective-permute-start.11) | collective-permute-done | bytes 65568 | tf_op jit(solution)/shard_map/ppermute | solution.py:13
  106.8 23.6 %psum.46 = bf16[256,16]{1,0:T(8,128)(2,1)S(1)} all-reduce(f32[256,16]{1,0:T(8,128)S(1)} %fusion.90), channel_id=1, replica_groups=mesh['head'=2,'outer'=4,'inner'=4] {'head','inner'}, use_global_device_ids=true, to_apply=%region_24.25 | all-reduce | flops 4096 | bytes 24576 | tf_op jit(solution)/shard_map/psum | solution.py:120
  130.4 6.5 %all-reduce.6.cloned.1.call-done = (bf16[256,1,128]{2,0,1:T(8,128)(2,1)}, bf16[256,128]{1,0:T(8,128)(2,1)}) async-done(((bf16[256,1,128]{2,0,1:T(8,128)(2,1)}, bf16[256,128]{1,0:T(8,128)(2,1)}), (bf16[256,1,128]{2,0,1:T(8,128)(2,1)}, bf16[256,128]{1,0:T(8,128)(2,1)})) %all-reduce.6.cloned.1.call-update) | async-done | bytes 131088 | tf_op jit(solution)/shard_map/psum | solution.py:190
  136.9 0.9 fusion.71
  137.9 9.9 %psum.44 = bf16[256,16]{1,0:T(8,128)(2,1)S(1)} all-reduce(f32[256,16]{1,0:T(8,128)S(1)} %fusion.89), channel_id=1, replica_groups=mesh['head'=2,'outer'=4,'inner'=4] {'head'}, use_global_device_ids=true, to_apply=%region_22.23 | all-reduce | flops 4096 | bytes 24576 | tf_op jit(solution)/shard_map/psum | solution.py:199
  147.8 0.8 convolution_bitcast_fusion.10
  148.9 12.7 %psum.47 = f32[16,128]{1,0:T(8,128)} all-reduce(f32[16,128]{1,0:T(8,128)S(1)} %fusion.91), channel_id=1, replica_groups=mesh['head'=2,'outer'=4,'inner'=4] {'outer'}, use_global_device_ids=true, to_apply=%region_25.26 | all-reduce | flops 2048 | bytes 16384 | tf_op jit(solution)/shard_map/psum | solution.py:206
  161.6 21.1 %all-reduce.4.cloned.1.call-done = f32[1024,16]{0,1:T(8,128)} async-done(((f32[1024,16]{0,1:T(8,128)}), f32[1024,16]{0,1:T(8,128)}) %all-reduce.4.cloned.1.call-update) | async-done | bytes 65552 | tf_op jit(solution)/shard_map/psum | solution.py:206
  (230 shorter events, 30.4 us)
Async XLA Ops:
  7.2 91.4 %copy-start = (bf16[256,1024]{1,0:T(8,128)(2,1)S(1)}, bf16[256,1024]{1,0:T(8,128)(2,1)}, u32[]{:S(2)}) copy-start(bf16[256,1024]{1,0:T(8,128)(2,1)} %param.25) | copy-start | bytes 1572868
  7.2 129.7 %all-reduce.6.cloned.1.call-start = ((), (), s32[]{:S(2)}) async-start(), calls=%async_computation.1 | async-start | bytes 262144 | tf_op jit(solution)/shard_map/psum | solution.py:190
  7.3 4.0 %copy-start.11 = (s32[1024]{0:T(1024)S(1)}, s32[1024]{0:T(1024)}, u32[]{:S(2)}) copy-start(s32[1024]{0:T(1024)} %param.29) | copy-start | bytes 12292
  7.3 0.7 copy-start.2
  7.3 5.5 %copy-start.3 = (bf16[256,256]{1,0:T(8,128)(2,1)S(1)}, bf16[256,256]{1,0:T(8,128)(2,1)}, u32[]{:S(2)}) copy-start(bf16[256,256]{1,0:T(8,128)(2,1)} %param.21) | copy-start | bytes 393220
  12.9 0.9 copy-start.4
  13.9 0.8 copy-start.9
  13.9 0.9 copy-start.10
  14.9 10.6 %collective-permute-start = (bf16[128,128]{1,0:T(8,128)(2,1)S(1)}, bf16[128,128]{1,0:T(8,128)(2,1)S(1)}, u32[]{:S(2)}, u32[]{:S(2)}) collective-permute-start(bf16[128,128]{1,0:T(8,128)(2,1)S(1)} %copy.63), channel_id=1, source_target_pairs={{0,4},{4,8},{8,12},{12,0},{1,5},{5,9},{9,13},{13,1},{2,6},{6,10},{... | collective-permute-start | bytes 98312 | tf_op jit(solution)/shard_map/while/body/eval_jaxpr/ppermute | solution.py:13
  18.1 7.5 %collective-permute-start.1 = (bf16[128,128]{1,0:T(8,128)(2,1)S(1)}, bf16[128,128]{1,0:T(8,128)(2,1)S(1)}, u32[]{:S(2)}, u32[]{:S(2)}) collective-permute-start(bf16[128,128]{1,0:T(8,128)(2,1)S(1)} %copy.64), channel_id=1, source_target_pairs={{0,4},{4,8},{8,12},{12,0},{1,5},{5,9},{9,13},{13,1},{2,6},{6,10},{... | collective-permute-start | bytes 98312 | tf_op jit(solution)/shard_map/while/body/eval_jaxpr/ppermute | solution.py:13
  19.6 6.0 %collective-permute-start.2 = (bf16[128,128]{1,0:T(8,128)(2,1)S(1)}, bf16[128,128]{1,0:T(8,128)(2,1)S(1)}, u32[]{:S(2)}, u32[]{:S(2)}) collective-permute-start(bf16[128,128]{1,0:T(8,128)(2,1)S(1)} %copy.65), channel_id=1, source_target_pairs={{0,4},{4,8},{8,12},{12,0},{1,5},{5,9},{9,13},{13,1},{2,6},{6,10},{... | collective-permute-start | bytes 98312 | tf_op jit(solution)/shard_map/while/body/eval_jaxpr/ppermute | solution.py:13
  21.2 5.7 %collective-permute-start.3 = (bf16[128,128]{1,0:T(8,128)(2,1)S(1)}, bf16[128,128]{1,0:T(8,128)(2,1)S(1)}, u32[]{:S(2)}, u32[]{:S(2)}) collective-permute-start(bf16[128,128]{1,0:T(8,128)(2,1)S(1)} %copy.66), channel_id=1, source_target_pairs={{0,4},{4,8},{8,12},{12,0},{1,5},{5,9},{9,13},{13,1},{2,6},{6,10},{... | collective-permute-start | bytes 98312 | tf_op jit(solution)/shard_map/while/body/eval_jaxpr/ppermute | solution.py:13
  26.9 9.2 %collective-permute-start = (bf16[128,128]{1,0:T(8,128)(2,1)S(1)}, bf16[128,128]{1,0:T(8,128)(2,1)S(1)}, u32[]{:S(2)}, u32[]{:S(2)}) collective-permute-start(bf16[128,128]{1,0:T(8,128)(2,1)S(1)} %copy.63), channel_id=1, source_target_pairs={{0,4},{4,8},{8,12},{12,0},{1,5},{5,9},{9,13},{13,1},{2,6},{6,10},{... | collective-permute-start | bytes 98312 | tf_op jit(solution)/shard_map/while/body/eval_jaxpr/ppermute | solution.py:13
  27.4 8.8 %collective-permute-start.1 = (bf16[128,128]{1,0:T(8,128)(2,1)S(1)}, bf16[128,128]{1,0:T(8,128)(2,1)S(1)}, u32[]{:S(2)}, u32[]{:S(2)}) collective-permute-start(bf16[128,128]{1,0:T(8,128)(2,1)S(1)} %copy.64), channel_id=1, source_target_pairs={{0,4},{4,8},{8,12},{12,0},{1,5},{5,9},{9,13},{13,1},{2,6},{6,10},{... | collective-permute-start | bytes 98312 | tf_op jit(solution)/shard_map/while/body/eval_jaxpr/ppermute | solution.py:13
  29.0 7.2 %collective-permute-start.2 = (bf16[128,128]{1,0:T(8,128)(2,1)S(1)}, bf16[128,128]{1,0:T(8,128)(2,1)S(1)}, u32[]{:S(2)}, u32[]{:S(2)}) collective-permute-start(bf16[128,128]{1,0:T(8,128)(2,1)S(1)} %copy.65), channel_id=1, source_target_pairs={{0,4},{4,8},{8,12},{12,0},{1,5},{5,9},{9,13},{13,1},{2,6},{6,10},{... | collective-permute-start | bytes 98312 | tf_op jit(solution)/shard_map/while/body/eval_jaxpr/ppermute | solution.py:13
  30.6 5.7 %collective-permute-start.3 = (bf16[128,128]{1,0:T(8,128)(2,1)S(1)}, bf16[128,128]{1,0:T(8,128)(2,1)S(1)}, u32[]{:S(2)}, u32[]{:S(2)}) collective-permute-start(bf16[128,128]{1,0:T(8,128)(2,1)S(1)} %copy.66), channel_id=1, source_target_pairs={{0,4},{4,8},{8,12},{12,0},{1,5},{5,9},{9,13},{13,1},{2,6},{6,10},{... | collective-permute-start | bytes 98312 | tf_op jit(solution)/shard_map/while/body/eval_jaxpr/ppermute | solution.py:13
  36.3 9.2 %collective-permute-start = (bf16[128,128]{1,0:T(8,128)(2,1)S(1)}, bf16[128,128]{1,0:T(8,128)(2,1)S(1)}, u32[]{:S(2)}, u32[]{:S(2)}) collective-permute-start(bf16[128,128]{1,0:T(8,128)(2,1)S(1)} %copy.63), channel_id=1, source_target_pairs={{0,4},{4,8},{8,12},{12,0},{1,5},{5,9},{9,13},{13,1},{2,6},{6,10},{... | collective-permute-start | bytes 98312 | tf_op jit(solution)/shard_map/while/body/eval_jaxpr/ppermute | solution.py:13
  36.8 8.8 %collective-permute-start.1 = (bf16[128,128]{1,0:T(8,128)(2,1)S(1)}, bf16[128,128]{1,0:T(8,128)(2,1)S(1)}, u32[]{:S(2)}, u32[]{:S(2)}) collective-permute-start(bf16[128,128]{1,0:T(8,128)(2,1)S(1)} %copy.64), channel_id=1, source_target_pairs={{0,4},{4,8},{8,12},{12,0},{1,5},{5,9},{9,13},{13,1},{2,6},{6,10},{... | collective-permute-start | bytes 98312 | tf_op jit(solution)/shard_map/while/body/eval_jaxpr/ppermute | solution.py:13
  38.4 7.2 %collective-permute-start.2 = (bf16[128,128]{1,0:T(8,128)(2,1)S(1)}, bf16[128,128]{1,0:T(8,128)(2,1)S(1)}, u32[]{:S(2)}, u32[]{:S(2)}) collective-permute-start(bf16[128,128]{1,0:T(8,128)(2,1)S(1)} %copy.65), channel_id=1, source_target_pairs={{0,4},{4,8},{8,12},{12,0},{1,5},{5,9},{9,13},{13,1},{2,6},{6,10},{... | collective-permute-start | bytes 98312 | tf_op jit(solution)/shard_map/while/body/eval_jaxpr/ppermute | solution.py:13
  39.9 5.7 %collective-permute-start.3 = (bf16[128,128]{1,0:T(8,128)(2,1)S(1)}, bf16[128,128]{1,0:T(8,128)(2,1)S(1)}, u32[]{:S(2)}, u32[]{:S(2)}) collective-permute-start(bf16[128,128]{1,0:T(8,128)(2,1)S(1)} %copy.66), channel_id=1, source_target_pairs={{0,4},{4,8},{8,12},{12,0},{1,5},{5,9},{9,13},{13,1},{2,6},{6,10},{... | collective-permute-start | bytes 98312 | tf_op jit(solution)/shard_map/while/body/eval_jaxpr/ppermute | solution.py:13
  51.6 6.5 %collective-permute-start.9 = (bf16[256,1,128]{2,0,1:T(8,128)(2,1)S(1)}, bf16[256,1,128]{2,0,1:T(8,128)(2,1)S(1)}, u32[]{:S(2)}, u32[]{:S(2)}) collective-permute-start(bf16[256,1,128]{2,0,1:T(8,128)(2,1)S(1)} %convert_element_type.175), channel_id=1, source_target_pairs={{0,4},{4,8},{8,12},{12,0},{1,5},{5,9},{9,13},{13,1},{2,6},{6,10},{... | collective-permute-start | bytes 196616 | tf_op jit(solution)/shard_map/while/body/eval_jaxpr/ppermute | solution.py:13
  51.7 7.1 %collective-permute-start.8 = (bf16[256,1,128]{2,0,1:T(8,128)(2,1)S(1)}, bf16[256,1,128]{2,0,1:T(8,128)(2,1)S(1)}, u32[]{:S(2)}, u32[]{:S(2)}) collective-permute-start(bf16[256,1,128]{2,0,1:T(8,128)(2,1)S(1)} %convert_element_type.173), channel_id=1, source_target_pairs={{0,4},{4,8},{8,12},{12,0},{1,5},{5,9},{9,13},{13,1},{2,6},{6,10},{... | collective-permute-start | bytes 196616 | tf_op jit(solution)/shard_map/while/body/eval_jaxpr/ppermute | solution.py:13
  52.9 6.2 %collective-permute-start.4 = (bf16[128,128]{1,0:T(8,128)(2,1)S(1)}, bf16[128,128]{1,0:T(8,128)(2,1)S(1)}, u32[]{:S(2)}, u32[]{:S(2)}) collective-permute-start(bf16[128,128]{1,0:T(8,128)(2,1)S(1)} %copy.95), channel_id=1, source_target_pairs={{0,4},{4,8},{8,12},{12,0},{1,5},{5,9},{9,13},{13,1},{2,6},{6,10},{... | collective-permute-start | bytes 98312 | tf_op jit(solution)/shard_map/while/body/eval_jaxpr/ppermute | solution.py:13
  54.6 5.7 %collective-permute-start.5 = (bf16[128,128]{1,0:T(8,128)(2,1)S(1)}, bf16[128,128]{1,0:T(8,128)(2,1)S(1)}, u32[]{:S(2)}, u32[]{:S(2)}) collective-permute-start(bf16[128,128]{1,0:T(8,128)(2,1)S(1)} %copy.96), channel_id=1, source_target_pairs={{0,4},{4,8},{8,12},{12,0},{1,5},{5,9},{9,13},{13,1},{2,6},{6,10},{... | collective-permute-start | bytes 98312 | tf_op jit(solution)/shard_map/while/body/eval_jaxpr/ppermute | solution.py:13
  56.7 5.7 %collective-permute-start.6 = (bf16[128,128]{1,0:T(8,128)(2,1)S(1)}, bf16[128,128]{1,0:T(8,128)(2,1)S(1)}, u32[]{:S(2)}, u32[]{:S(2)}) collective-permute-start(bf16[128,128]{1,0:T(8,128)(2,1)S(1)} %copy.97), channel_id=1, source_target_pairs={{0,4},{4,8},{8,12},{12,0},{1,5},{5,9},{9,13},{13,1},{2,6},{6,10},{... | collective-permute-start | bytes 98312 | tf_op jit(solution)/shard_map/while/body/eval_jaxpr/ppermute | solution.py:13
  58.1 5.7 %collective-permute-start.7 = (bf16[128,128]{1,0:T(8,128)(2,1)S(1)}, bf16[128,128]{1,0:T(8,128)(2,1)S(1)}, u32[]{:S(2)}, u32[]{:S(2)}) collective-permute-start(bf16[128,128]{1,0:T(8,128)(2,1)S(1)} %copy.98), channel_id=1, source_target_pairs={{0,4},{4,8},{8,12},{12,0},{1,5},{5,9},{9,13},{13,1},{2,6},{6,10},{... | collective-permute-start | bytes 98312 | tf_op jit(solution)/shard_map/while/body/eval_jaxpr/ppermute | solution.py:13
  68.6 6.1 %collective-permute-start.9 = (bf16[256,1,128]{2,0,1:T(8,128)(2,1)S(1)}, bf16[256,1,128]{2,0,1:T(8,128)(2,1)S(1)}, u32[]{:S(2)}, u32[]{:S(2)}) collective-permute-start(bf16[256,1,128]{2,0,1:T(8,128)(2,1)S(1)} %convert_element_type.175), channel_id=1, source_target_pairs={{0,4},{4,8},{8,12},{12,0},{1,5},{5,9},{9,13},{13,1},{2,6},{6,10},{... | collective-permute-start | bytes 196616 | tf_op jit(solution)/shard_map/while/body/eval_jaxpr/ppermute | solution.py:13
  68.7 6.7 %collective-permute-start.8 = (bf16[256,1,128]{2,0,1:T(8,128)(2,1)S(1)}, bf16[256,1,128]{2,0,1:T(8,128)(2,1)S(1)}, u32[]{:S(2)}, u32[]{:S(2)}) collective-permute-start(bf16[256,1,128]{2,0,1:T(8,128)(2,1)S(1)} %convert_element_type.173), channel_id=1, source_target_pairs={{0,4},{4,8},{8,12},{12,0},{1,5},{5,9},{9,13},{13,1},{2,6},{6,10},{... | collective-permute-start | bytes 196616 | tf_op jit(solution)/shard_map/while/body/eval_jaxpr/ppermute | solution.py:13
  68.8 7.0 %collective-permute-start.4 = (bf16[128,128]{1,0:T(8,128)(2,1)S(1)}, bf16[128,128]{1,0:T(8,128)(2,1)S(1)}, u32[]{:S(2)}, u32[]{:S(2)}) collective-permute-start(bf16[128,128]{1,0:T(8,128)(2,1)S(1)} %copy.95), channel_id=1, source_target_pairs={{0,4},{4,8},{8,12},{12,0},{1,5},{5,9},{9,13},{13,1},{2,6},{6,10},{... | collective-permute-start | bytes 98312 | tf_op jit(solution)/shard_map/while/body/eval_jaxpr/ppermute | solution.py:13
  70.5 5.7 %collective-permute-start.5 = (bf16[128,128]{1,0:T(8,128)(2,1)S(1)}, bf16[128,128]{1,0:T(8,128)(2,1)S(1)}, u32[]{:S(2)}, u32[]{:S(2)}) collective-permute-start(bf16[128,128]{1,0:T(8,128)(2,1)S(1)} %copy.96), channel_id=1, source_target_pairs={{0,4},{4,8},{8,12},{12,0},{1,5},{5,9},{9,13},{13,1},{2,6},{6,10},{... | collective-permute-start | bytes 98312 | tf_op jit(solution)/shard_map/while/body/eval_jaxpr/ppermute | solution.py:13
  73.7 5.7 %collective-permute-start.6 = (bf16[128,128]{1,0:T(8,128)(2,1)S(1)}, bf16[128,128]{1,0:T(8,128)(2,1)S(1)}, u32[]{:S(2)}, u32[]{:S(2)}) collective-permute-start(bf16[128,128]{1,0:T(8,128)(2,1)S(1)} %copy.97), channel_id=1, source_target_pairs={{0,4},{4,8},{8,12},{12,0},{1,5},{5,9},{9,13},{13,1},{2,6},{6,10},{... | collective-permute-start | bytes 98312 | tf_op jit(solution)/shard_map/while/body/eval_jaxpr/ppermute | solution.py:13
  74.8 5.7 %collective-permute-start.7 = (bf16[128,128]{1,0:T(8,128)(2,1)S(1)}, bf16[128,128]{1,0:T(8,128)(2,1)S(1)}, u32[]{:S(2)}, u32[]{:S(2)}) collective-permute-start(bf16[128,128]{1,0:T(8,128)(2,1)S(1)} %copy.98), channel_id=1, source_target_pairs={{0,4},{4,8},{8,12},{12,0},{1,5},{5,9},{9,13},{13,1},{2,6},{6,10},{... | collective-permute-start | bytes 98312 | tf_op jit(solution)/shard_map/while/body/eval_jaxpr/ppermute | solution.py:13
  85.3 6.1 %collective-permute-start.9 = (bf16[256,1,128]{2,0,1:T(8,128)(2,1)S(1)}, bf16[256,1,128]{2,0,1:T(8,128)(2,1)S(1)}, u32[]{:S(2)}, u32[]{:S(2)}) collective-permute-start(bf16[256,1,128]{2,0,1:T(8,128)(2,1)S(1)} %convert_element_type.175), channel_id=1, source_target_pairs={{0,4},{4,8},{8,12},{12,0},{1,5},{5,9},{9,13},{13,1},{2,6},{6,10},{... | collective-permute-start | bytes 196616 | tf_op jit(solution)/shard_map/while/body/eval_jaxpr/ppermute | solution.py:13
  85.4 6.7 %collective-permute-start.8 = (bf16[256,1,128]{2,0,1:T(8,128)(2,1)S(1)}, bf16[256,1,128]{2,0,1:T(8,128)(2,1)S(1)}, u32[]{:S(2)}, u32[]{:S(2)}) collective-permute-start(bf16[256,1,128]{2,0,1:T(8,128)(2,1)S(1)} %convert_element_type.173), channel_id=1, source_target_pairs={{0,4},{4,8},{8,12},{12,0},{1,5},{5,9},{9,13},{13,1},{2,6},{6,10},{... | collective-permute-start | bytes 196616 | tf_op jit(solution)/shard_map/while/body/eval_jaxpr/ppermute | solution.py:13
  85.5 7.2 %collective-permute-start.4 = (bf16[128,128]{1,0:T(8,128)(2,1)S(1)}, bf16[128,128]{1,0:T(8,128)(2,1)S(1)}, u32[]{:S(2)}, u32[]{:S(2)}) collective-permute-start(bf16[128,128]{1,0:T(8,128)(2,1)S(1)} %copy.95), channel_id=1, source_target_pairs={{0,4},{4,8},{8,12},{12,0},{1,5},{5,9},{9,13},{13,1},{2,6},{6,10},{... | collective-permute-start | bytes 98312 | tf_op jit(solution)/shard_map/while/body/eval_jaxpr/ppermute | solution.py:13
  87.9 6.1 %collective-permute-start.5 = (bf16[128,128]{1,0:T(8,128)(2,1)S(1)}, bf16[128,128]{1,0:T(8,128)(2,1)S(1)}, u32[]{:S(2)}, u32[]{:S(2)}) collective-permute-start(bf16[128,128]{1,0:T(8,128)(2,1)S(1)} %copy.96), channel_id=1, source_target_pairs={{0,4},{4,8},{8,12},{12,0},{1,5},{5,9},{9,13},{13,1},{2,6},{6,10},{... | collective-permute-start | bytes 98312 | tf_op jit(solution)/shard_map/while/body/eval_jaxpr/ppermute | solution.py:13
  90.4 5.7 %collective-permute-start.6 = (bf16[128,128]{1,0:T(8,128)(2,1)S(1)}, bf16[128,128]{1,0:T(8,128)(2,1)S(1)}, u32[]{:S(2)}, u32[]{:S(2)}) collective-permute-start(bf16[128,128]{1,0:T(8,128)(2,1)S(1)} %copy.97), channel_id=1, source_target_pairs={{0,4},{4,8},{8,12},{12,0},{1,5},{5,9},{9,13},{13,1},{2,6},{6,10},{... | collective-permute-start | bytes 98312 | tf_op jit(solution)/shard_map/while/body/eval_jaxpr/ppermute | solution.py:13
  91.4 5.7 %collective-permute-start.7 = (bf16[128,128]{1,0:T(8,128)(2,1)S(1)}, bf16[128,128]{1,0:T(8,128)(2,1)S(1)}, u32[]{:S(2)}, u32[]{:S(2)}) collective-permute-start(bf16[128,128]{1,0:T(8,128)(2,1)S(1)} %copy.98), channel_id=1, source_target_pairs={{0,4},{4,8},{8,12},{12,0},{1,5},{5,9},{9,13},{13,1},{2,6},{6,10},{... | collective-permute-start | bytes 98312 | tf_op jit(solution)/shard_map/while/body/eval_jaxpr/ppermute | solution.py:13
  98.4 6.1 %collective-permute-start.11 = (bf16[256,1,128]{2,0,1:T(8,128)(2,1)S(1)}, bf16[256,1,128]{2,0,1:T(8,128)(2,1)S(1)}, u32[]{:S(2)}, u32[]{:S(2)}) collective-permute-start(bf16[256,1,128]{2,0,1:T(8,128)(2,1)S(1)} %convert_element_type.122), channel_id=1, source_target_pairs={{0,4},{4,8},{8,12},{12,0},{1,5},{5,9},{9,13},{13,1},{2,6},{6,10},{... | collective-permute-start | bytes 196616 | tf_op jit(solution)/shard_map/ppermute | solution.py:13
  98.5 0.8 copy-start.12
  98.5 6.7 %collective-permute-start.10 = (bf16[256,1,128]{2,0,1:T(8,128)(2,1)S(1)}, bf16[256,1,128]{2,0,1:T(8,128)(2,1)S(1)}, u32[]{:S(2)}, u32[]{:S(2)}) collective-permute-start(bf16[256,1,128]{2,0,1:T(8,128)(2,1)S(1)} %convert_element_type.119), channel_id=1, source_target_pairs={{0,4},{4,8},{8,12},{12,0},{1,5},{5,9},{9,13},{13,1},{2,6},{6,10},{... | collective-permute-start | bytes 196616 | tf_op jit(solution)/shard_map/ppermute | solution.py:13
  104.5 0.7 copy-start.6
  105.2 0.6 copy-start.7
  105.9 76.8 %all-reduce.4.cloned.1.call-start = ((), (), s32[]{:S(2)}) async-start(), calls=%async_computation | async-start | bytes 131072 | tf_op jit(solution)/shard_map/psum | solution.py:206
  136.9 0.9 copy-start.13
  137.8 10.9 %copy-start.1 = (bf16[256,128]{1,0:T(8,128)(2,1)}, bf16[256,128]{1,0:T(8,128)(2,1)S(1)}, u32[]{:S(2)}) copy-start(bf16[256,128]{1,0:T(8,128)(2,1)S(1)} %fusion.71) | copy-start | bytes 196612
  148.7 34.0 %copy-start.5 = (bf16[256,128]{1,0:T(8,128)(2,1)S(1)}, bf16[256,128]{1,0:T(8,128)(2,1)}, u32[]{:S(2)}) copy-start(bf16[256,128]{1,0:T(8,128)(2,1)} %get-tuple-element.1577) | copy-start | bytes 196612
  182.7 0.9 copy-start.8
Sparse Core Ops, SparseCore 0:
  106.0 30.8 all-reduce.5
  148.8 33.8 all-reduce.3
where the time goes:
time: 192 us; the launch traced here: 191 us
  waiting for transfers between devices  55.2 us (29%)
  blocking collectives  46.2 us (24%)
  starting transfers between devices  31.7 us (17%)
  between operations  17.7 us (9%)
  loops' own time  12.8 us (7%)
  local copies, waits for them, and re-layouts  11.2 us (6%)
  matrix products  8.69 us (5%)
  other arithmetic  7.44 us (4%)
    ppermute x32, starting transfers between devices, passed_along(): return lax.ppermute(value, axis, pairs)  31.7 us
    ppermute x32, waiting for transfers between devices, passed_along(): return lax.ppermute(value, axis, pairs)  27.6 us
    psum x1, blocking collectives, on_device(): low_rank = lax.psum(low_partial, ('head', 'inner')).astype(jnp.bfloat16)  23.6 us
    psum x1, waiting for transfers between devices, on_device(): grad_a, grad_b = lax.psum((grad_a_part, grad_b_part), 'outer')  21.1 us
    psum x1, blocking collectives, on_device(): grad_a, grad_b = lax.psum((grad_a_part, grad_b_part), 'outer')  12.7 us
    psum x1, blocking collectives, on_device(): back_rank = lax.psum(back_partial, 'head').astype(jnp.bfloat16)  9.87 us
    psum x1, waiting for transfers between devices, on_device(): lax.psum(key_acc.astype(jnp.bfloat16), 'inner').astype(jnp.float32)  6.49 us
    another operation x1, loops' own time, on_device(): lax.fori_loop(0, cycle_size - 1, backward_turn, (local_keys, (empty_query...  6.29 us
  transfers between devices with their start and end apart: 34, of which 25 were waited for; matrix products, arithmetic and copies ran while one was open for 4% of the time, Pallas kernels for 0%

commit v1 on v0

--- a/solution.py
+++ b/solution.py
@@ -1,10 +1,21 @@
+import functools
 import jax
 import jax.numpy as jnp
 from jax import lax
 from jax.sharding import PartitionSpec as P
+from jax.lax import psum
 
 HEAD_DIM = 128
 NEGATIVE = -1e30
+
+
+def _supply_all_turns(vector, along_axis, mesh_name):
+    for num in (along_axis, mesh_name):
+        vector = psum(vector, axis_name=num)
+    return vector
+
+
+process_side_now = functools.partial(_supply_all_turns, along_axis="head", mesh_name="inner")
 
 
 def passed_along(value, axis, steps):
@@ -117,7 +128,7 @@
     )
     local_keys = (keys[:half_rows], values[:half_rows], keys[half_rows:], values[half_rows:])
     low_partial = jnp.dot(hidden_in, adapter_a, preferred_element_type=jnp.float32)
-    low_rank = lax.psum(low_partial, ("head", "inner")).astype(jnp.bfloat16)
+    low_rank = process_side_now(low_partial).astype(jnp.bfloat16)
 
     def sweep(counter, current, handle, carried):
         upper_src, lower_src = anchors(member, cycle_size, counter)

time: 192 us -> 206 us (1.073)
  waiting for transfers between devices: 55.2 us -> 78.7 us
  blocking collectives: 46.2 us -> 36.3 us
    psum x1, waiting for transfers between devices: 6.49 us -> 30.1 us  [on_device(): lax.psum(key_acc.astype(jnp.bfloat16), 'inner').astype(jnp.float32)]
    psum x1, blocking collectives: 23.6 us -> 11.7 us  [_supply_all_turns(): vector = psum(vector, axis_name=num)]
    psum x1, blocking collectives: 9.87 us -> 12.4 us  [on_device(): back_rank = lax.psum(back_partial, 'head').astype(jnp.bfloat16)]
    unnamed x39 -> x35, local copies, waits for them, and re-layouts: 6.13 us -> 6.14 us
where the time goes in v1:
time: 206 us; the launch traced here: 205 us
  waiting for transfers between devices  78.7 us (38%)
  blocking collectives  36.3 us (18%)
  starting transfers between devices  31.8 us (15%)
  between operations  17.7 us (9%)
  loops' own time  12.8 us (6%)
  local copies, waits for them, and re-layouts  12.1 us (6%)
  matrix products  8.7 us (4%)
  other arithmetic  7.44 us (4%)
    ppermute x32, starting transfers between devices, passed_along(): return lax.ppermute(value, axis, pairs)  31.7 us
    psum x1, waiting for transfers between devices, on_device(): lax.psum(key_acc.astype(jnp.bfloat16), 'inner').astype(jnp.float32)  30.1 us
    ppermute x32, waiting for transfers between devices, passed_along(): return lax.ppermute(value, axis, pairs)  27.6 us
    psum x1, waiting for transfers between devices, on_device(): grad_a, grad_b = lax.psum((grad_a_part, grad_b_part), 'outer')  21 us
    psum x1, blocking collectives, on_device(): back_rank = lax.psum(back_partial, 'head').astype(jnp.bfloat16)  12.4 us
    psum x1, blocking collectives, on_device(): grad_a, grad_b = lax.psum((grad_a_part, grad_b_part), 'outer')  12.2 us
    psum x1, blocking collectives, _supply_all_turns(): vector = psum(vector, axis_name=num)  11.7 us
    another operation x1, loops' own time, on_device(): lax.fori_loop(0, cycle_size - 1, backward_turn, (local_keys, (empty_query...  6.31 us
  transfers between devices with their start and end apart: 34, of which 25 were waited for; matrix products, arithmetic and copies ran while one was open for 4% of the time, Pallas kernels for 0%

profile of v1, /device:TPU:0, one launch (start us, length us, event | category | flops | bytes accessed | tf_op | source)
XLA Modules:
  0.0 205.4 jit_solution(12089945055986489718)
XLA Ops:
  11.2 0.8 fusion.85
  12.1 0.8 copy-done.3
  15.7 30.7 %while.55 = (s32[]{:T(128)}, bf16[128,128]{1,0:T(8,128)(2,1)S(1)}, bf16[128,128]{1,0:T(8,128)(2,1)S(1)}, bf16[128,128]{1,0:T(8,128)(2,1)S(1)}, bf16[128,128]{1,0...) while((s32[]{:T(128)}, bf16[128,128]{1,0:T(8,128)(2,1)S(1)}, ...), condition=%wide.region_7.8_spmd, body=%wide.region_1.7_spmd.sunk | while | flops 68946208 | bytes 3714876 | solution.py:165
  15.7 3.1 %collective-permute-start = (bf16[128,128]{1,0:T(8,128)(2,1)S(1)}, bf16[128,128]{1,0:T(8,128)(2,1)S(1)}, u32[]{:S(2)}, u32[]{:S(2)}) collective-permute-start(bf16[128,128]{1,0:T(8,128)(2,1)S(1)} %copy.63), channel_id=1, source_target_pairs={{0,4},{4,8},{8,12},{12,0},{1,5},{5,9},{9,13},{13,1},{2,6},{6,10},{... | collective-permute-start | bytes 98312 | tf_op jit(solution)/shard_map/while/body/eval_jaxpr/ppermute | solution.py:24
  18.8 1.6 collective-permute-start.1
  20.4 1.6 collective-permute-start.2
  25.5 0.8 conditional.9
  26.4 1.3 collective-permute-done.3
  28.2 1.6 collective-permute-start.1
  29.8 1.6 collective-permute-start.2
  31.4 1.3 collective-permute-start.3
  36.1 0.8 conditional.9
  37.6 1.6 collective-permute-start.1
  39.2 1.6 collective-permute-start.2
  40.7 1.3 collective-permute-start.3
  45.5 0.8 conditional.9
  46.5 0.9 conditional.4
  47.5 50.4 %while.56 = (s32[]{:T(128)}, bf16[128,128]{1,0:T(8,128)(2,1)S(1)}, bf16[128,128]{1,0:T(8,128)(2,1)S(1)}, bf16[128,128]{1,0:T(8,128)(2,1)S(1)}, bf16[128,128]{1,0...) while((s32[]{:T(128)}, bf16[128,128]{1,0:T(8,128)(2,1)S(1)}, ...), condition=%wide.region_17.18_spmd.clone, body=%wide.region_13.17_spmd.clone.sunk | while | flops 169542432 | bytes 7159750 | solution.py:195
  51.1 1.3 conditional.10
  52.5 1.2 collective-permute-start.9
  53.7 1.6 collective-permute-start.4
  55.3 2.1 %collective-permute-start.5 = (bf16[128,128]{1,0:T(8,128)(2,1)S(1)}, bf16[128,128]{1,0:T(8,128)(2,1)S(1)}, u32[]{:S(2)}, u32[]{:S(2)}) collective-permute-start(bf16[128,128]{1,0:T(8,128)(2,1)S(1)} %copy.96), channel_id=1, source_target_pairs={{0,4},{4,8},{8,12},{12,0},{1,5},{5,9},{9,13},{13,1},{2,6},{6,10},{... | collective-permute-start | bytes 98312 | tf_op jit(solution)/shard_map/while/body/eval_jaxpr/ppermute | solution.py:24
  57.5 1.3 collective-permute-done.8
  59.9 1.1 collective-permute-done.5
  61.1 2.1 %collective-permute-done.6 = bf16[128,128]{1,0:T(8,128)(2,1)S(1)} collective-permute-done((bf16[128,128]{1,0:T(8,128)(2,1)S(1)}, bf16[128,128]{1,0:T(8,128)(2,1)S(1)}, u32[]{:S(2)}, u32[]{:S(2)}) %collective-permute-start.6) | collective-permute-done | bytes 32800 | tf_op jit(solution)/shard_map/while/body/eval_jaxpr/ppermute | solution.py:24
  63.2 1.4 collective-permute-done.7
  68.1 1.3 conditional.10
  69.6 1.7 collective-permute-start.4
  71.3 3.2 %collective-permute-start.5 = (bf16[128,128]{1,0:T(8,128)(2,1)S(1)}, bf16[128,128]{1,0:T(8,128)(2,1)S(1)}, u32[]{:S(2)}, u32[]{:S(2)}) collective-permute-start(bf16[128,128]{1,0:T(8,128)(2,1)S(1)} %copy.96), channel_id=1, source_target_pairs={{0,4},{4,8},{8,12},{12,0},{1,5},{5,9},{9,13},{13,1},{2,6},{6,10},{... | collective-permute-start | bytes 98312 | tf_op jit(solution)/shard_map/while/body/eval_jaxpr/ppermute | solution.py:24
  74.6 1.0 collective-permute-done.8
  77.0 3.2 %collective-permute-done.6 = bf16[128,128]{1,0:T(8,128)(2,1)S(1)} collective-permute-done((bf16[128,128]{1,0:T(8,128)(2,1)S(1)}, bf16[128,128]{1,0:T(8,128)(2,1)S(1)}, u32[]{:S(2)}, u32[]{:S(2)}) %collective-permute-start.6) | collective-permute-done | bytes 32800 | tf_op jit(solution)/shard_map/while/body/eval_jaxpr/ppermute | solution.py:24
  80.2 1.0 collective-permute-done.7
  84.8 1.3 conditional.10
  86.3 2.4 %collective-permute-start.4 = (bf16[128,128]{1,0:T(8,128)(2,1)S(1)}, bf16[128,128]{1,0:T(8,128)(2,1)S(1)}, u32[]{:S(2)}, u32[]{:S(2)}) collective-permute-start(bf16[128,128]{1,0:T(8,128)(2,1)S(1)} %copy.95), channel_id=1, source_target_pairs={{0,4},{4,8},{8,12},{12,0},{1,5},{5,9},{9,13},{13,1},{2,6},{6,10},{... | collective-permute-start | bytes 98312 | tf_op jit(solution)/shard_map/while/body/eval_jaxpr/ppermute | solution.py:24
  88.7 2.5 %collective-permute-start.5 = (bf16[128,128]{1,0:T(8,128)(2,1)S(1)}, bf16[128,128]{1,0:T(8,128)(2,1)S(1)}, u32[]{:S(2)}, u32[]{:S(2)}) collective-permute-start(bf16[128,128]{1,0:T(8,128)(2,1)S(1)} %copy.96), channel_id=1, source_target_pairs={{0,4},{4,8},{8,12},{12,0},{1,5},{5,9},{9,13},{13,1},{2,6},{6,10},{... | collective-permute-start | bytes 98312 | tf_op jit(solution)/shard_map/while/body/eval_jaxpr/ppermute | solution.py:24
  91.2 1.0 collective-permute-done.8
  93.4 1.3 collective-permute-done.5
  94.7 2.1 %collective-permute-done.6 = bf16[128,128]{1,0:T(8,128)(2,1)S(1)} collective-permute-done((bf16[128,128]{1,0:T(8,128)(2,1)S(1)}, bf16[128,128]{1,0:T(8,128)(2,1)S(1)}, u32[]{:S(2)}, u32[]{:S(2)}) %collective-permute-start.6) | collective-permute-done | bytes 32800 | tf_op jit(solution)/shard_map/while/body/eval_jaxpr/ppermute | solution.py:24
  96.9 1.0 collective-permute-done.7
  98.0 1.2 conditional.5
  100.3 5.0 %collective-permute-done.11 = bf16[256,1,128]{2,0,1:T(8,128)(2,1)S(1)} collective-permute-done((bf16[256,1,128]{2,0,1:T(8,128)(2,1)S(1)}, bf16[256,1,128]{2,0,1:T(8,128)(2,1)S(1)}, u32[]{:S(2)}, u32[]{:S(2)}) %collective-permute-start.11) | collective-permute-done | bytes 65568 | tf_op jit(solution)/shard_map/ppermute | solution.py:24
  107.6 30.1 %all-reduce.7.cloned.1.call-done = (bf16[256,1,128]{2,0,1:T(8,128)(2,1)}, bf16[256,128]{1,0:T(8,128)(2,1)}) async-done(((bf16[256,1,128]{2,0,1:T(8,128)(2,1)}, bf16[256,128]{1,0:T(8,128)(2,1)}), (bf16[256,1,128]{2,0,1:T(8,128)(2,1)}, bf16[256,128]{1,0:T(8,128)(2,1)})) %all-reduce.7.cloned.1.call-update) | async-done | bytes 131088 | tf_op jit(solution)/shard_map/psum | solution.py:201
  137.8 0.9 fusion.71
  138.8 12.4 %all-reduce = (bf16[256,16]{1,0:T(8,128)(2,1)S(1)}, f32[256,16]{1,0:T(8,128)S(1)}) all-reduce(f32[256,16]{1,0:T(8,128)S(1)} %fusion.89, f32[256,16]{1,0:T(8,128)S(1)} %fusion.90), channel_id=1, replica_groups=mesh['head'=2,'outer'=4,'inner'=4] {'head'}, use_global_device_ids=true, to_apply=%region_22.23 | all-reduce | flops 8192 | bytes 57344 | tf_op jit(solution)/shard_map/psum | solution.py:210
  151.2 11.7 %psum.54 = bf16[256,16]{1,0:T(8,128)(2,1)S(1)} all-reduce(f32[256,16]{1,0:T(8,128)S(1)} %get-tuple-element.1098), channel_id=1, replica_groups=mesh['head'=2,'outer'=4,'inner'=4] {'inner'}, use_global_device_ids=true, to_apply=%region_25.26 | all-reduce | flops 4096 | bytes 24576 | tf_op jit(solution)/shard_map/psum | solution.py:14
  162.9 0.8 convolution_bitcast_fusion.10
  163.9 12.2 %psum.55 = f32[16,128]{1,0:T(8,128)} all-reduce(f32[16,128]{1,0:T(8,128)S(1)} %fusion.91), channel_id=1, replica_groups=mesh['head'=2,'outer'=4,'inner'=4] {'outer'}, use_global_device_ids=true, to_apply=%region_26.27 | all-reduce | flops 2048 | bytes 16384 | tf_op jit(solution)/shard_map/psum | solution.py:217
  176.1 21.0 %all-reduce.5.cloned.1.call-done = f32[1024,16]{0,1:T(8,128)} async-done(((f32[1024,16]{0,1:T(8,128)}), f32[1024,16]{0,1:T(8,128)}) %all-reduce.5.cloned.1.call-update) | async-done | bytes 65552 | tf_op jit(solution)/shard_map/psum | solution.py:217
  (226 shorter events, 31.1 us)
Async XLA Ops:
  7.2 92.2 %copy-start = (bf16[256,1024]{1,0:T(8,128)(2,1)S(1)}, bf16[256,1024]{1,0:T(8,128)(2,1)}, u32[]{:S(2)}) copy-start(bf16[256,1024]{1,0:T(8,128)(2,1)} %param.25) | copy-start | bytes 1572868
  7.2 130.6 %all-reduce.7.cloned.1.call-start = ((), (), s32[]{:S(2)}) async-start(), calls=%async_computation.1 | async-start | bytes 262144 | tf_op jit(solution)/shard_map/psum | solution.py:201
  7.3 0.7 copy-start.2
  12.0 0.9 copy-start.3
  13.0 2.4 %copy-start.4 = (bf16[256,256]{1,0:T(8,128)(2,1)S(1)}, bf16[256,256]{1,0:T(8,128)(2,1)}, u32[]{:S(2)}) copy-start(bf16[256,256]{1,0:T(8,128)(2,1)} %param.24) | copy-start | bytes 393220
  13.2 0.7 copy-start.9
  15.7 10.6 %collective-permute-start = (bf16[128,128]{1,0:T(8,128)(2,1)S(1)}, bf16[128,128]{1,0:T(8,128)(2,1)S(1)}, u32[]{:S(2)}, u32[]{:S(2)}) collective-permute-start(bf16[128,128]{1,0:T(8,128)(2,1)S(1)} %copy.63), channel_id=1, source_target_pairs={{0,4},{4,8},{8,12},{12,0},{1,5},{5,9},{9,13},{13,1},{2,6},{6,10},{... | collective-permute-start | bytes 98312 | tf_op jit(solution)/shard_map/while/body/eval_jaxpr/ppermute | solution.py:24
  18.8 7.5 %collective-permute-start.1 = (bf16[128,128]{1,0:T(8,128)(2,1)S(1)}, bf16[128,128]{1,0:T(8,128)(2,1)S(1)}, u32[]{:S(2)}, u32[]{:S(2)}) collective-permute-start(bf16[128,128]{1,0:T(8,128)(2,1)S(1)} %copy.64), channel_id=1, source_target_pairs={{0,4},{4,8},{8,12},{12,0},{1,5},{5,9},{9,13},{13,1},{2,6},{6,10},{... | collective-permute-start | bytes 98312 | tf_op jit(solution)/shard_map/while/body/eval_jaxpr/ppermute | solution.py:24
  20.4 6.0 %collective-permute-start.2 = (bf16[128,128]{1,0:T(8,128)(2,1)S(1)}, bf16[128,128]{1,0:T(8,128)(2,1)S(1)}, u32[]{:S(2)}, u32[]{:S(2)}) collective-permute-start(bf16[128,128]{1,0:T(8,128)(2,1)S(1)} %copy.65), channel_id=1, source_target_pairs={{0,4},{4,8},{8,12},{12,0},{1,5},{5,9},{9,13},{13,1},{2,6},{6,10},{... | collective-permute-start | bytes 98312 | tf_op jit(solution)/shard_map/while/body/eval_jaxpr/ppermute | solution.py:24
  22.0 5.7 %collective-permute-start.3 = (bf16[128,128]{1,0:T(8,128)(2,1)S(1)}, bf16[128,128]{1,0:T(8,128)(2,1)S(1)}, u32[]{:S(2)}, u32[]{:S(2)}) collective-permute-start(bf16[128,128]{1,0:T(8,128)(2,1)S(1)} %copy.66), channel_id=1, source_target_pairs={{0,4},{4,8},{8,12},{12,0},{1,5},{5,9},{9,13},{13,1},{2,6},{6,10},{... | collective-permute-start | bytes 98312 | tf_op jit(solution)/shard_map/while/body/eval_jaxpr/ppermute | solution.py:24
  27.7 9.2 %collective-permute-start = (bf16[128,128]{1,0:T(8,128)(2,1)S(1)}, bf16[128,128]{1,0:T(8,128)(2,1)S(1)}, u32[]{:S(2)}, u32[]{:S(2)}) collective-permute-start(bf16[128,128]{1,0:T(8,128)(2,1)S(1)} %copy.63), channel_id=1, source_target_pairs={{0,4},{4,8},{8,12},{12,0},{1,5},{5,9},{9,13},{13,1},{2,6},{6,10},{... | collective-permute-start | bytes 98312 | tf_op jit(solution)/shard_map/while/body/eval_jaxpr/ppermute | solution.py:24
  28.2 8.8 %collective-permute-start.1 = (bf16[128,128]{1,0:T(8,128)(2,1)S(1)}, bf16[128,128]{1,0:T(8,128)(2,1)S(1)}, u32[]{:S(2)}, u32[]{:S(2)}) collective-permute-start(bf16[128,128]{1,0:T(8,128)(2,1)S(1)} %copy.64), channel_id=1, source_target_pairs={{0,4},{4,8},{8,12},{12,0},{1,5},{5,9},{9,13},{13,1},{2,6},{6,10},{... | collective-permute-start | bytes 98312 | tf_op jit(solution)/shard_map/while/body/eval_jaxpr/ppermute | solution.py:24
  29.8 7.2 %collective-permute-start.2 = (bf16[128,128]{1,0:T(8,128)(2,1)S(1)}, bf16[128,128]{1,0:T(8,128)(2,1)S(1)}, u32[]{:S(2)}, u32[]{:S(2)}) collective-permute-start(bf16[128,128]{1,0:T(8,128)(2,1)S(1)} %copy.65), channel_id=1, source_target_pairs={{0,4},{4,8},{8,12},{12,0},{1,5},{5,9},{9,13},{13,1},{2,6},{6,10},{... | collective-permute-start | bytes 98312 | tf_op jit(solution)/shard_map/while/body/eval_jaxpr/ppermute | solution.py:24
  31.4 5.7 %collective-permute-start.3 = (bf16[128,128]{1,0:T(8,128)(2,1)S(1)}, bf16[128,128]{1,0:T(8,128)(2,1)S(1)}, u32[]{:S(2)}, u32[]{:S(2)}) collective-permute-start(bf16[128,128]{1,0:T(8,128)(2,1)S(1)} %copy.66), channel_id=1, source_target_pairs={{0,4},{4,8},{8,12},{12,0},{1,5},{5,9},{9,13},{13,1},{2,6},{6,10},{... | collective-permute-start | bytes 98312 | tf_op jit(solution)/shard_map/while/body/eval_jaxpr/ppermute | solution.py:24
  37.1 9.2 %collective-permute-start = (bf16[128,128]{1,0:T(8,128)(2,1)S(1)}, bf16[128,128]{1,0:T(8,128)(2,1)S(1)}, u32[]{:S(2)}, u32[]{:S(2)}) collective-permute-start(bf16[128,128]{1,0:T(8,128)(2,1)S(1)} %copy.63), channel_id=1, source_target_pairs={{0,4},{4,8},{8,12},{12,0},{1,5},{5,9},{9,13},{13,1},{2,6},{6,10},{... | collective-permute-start | bytes 98312 | tf_op jit(solution)/shard_map/while/body/eval_jaxpr/ppermute | solution.py:24
  37.6 8.8 %collective-permute-start.1 = (bf16[128,128]{1,0:T(8,128)(2,1)S(1)}, bf16[128,128]{1,0:T(8,128)(2,1)S(1)}, u32[]{:S(2)}, u32[]{:S(2)}) collective-permute-start(bf16[128,128]{1,0:T(8,128)(2,1)S(1)} %copy.64), channel_id=1, source_target_pairs={{0,4},{4,8},{8,12},{12,0},{1,5},{5,9},{9,13},{13,1},{2,6},{6,10},{... | collective-permute-start | bytes 98312 | tf_op jit(solution)/shard_map/while/body/eval_jaxpr/ppermute | solution.py:24
  39.2 7.2 %collective-permute-start.2 = (bf16[128,128]{1,0:T(8,128)(2,1)S(1)}, bf16[128,128]{1,0:T(8,128)(2,1)S(1)}, u32[]{:S(2)}, u32[]{:S(2)}) collective-permute-start(bf16[128,128]{1,0:T(8,128)(2,1)S(1)} %copy.65), channel_id=1, source_target_pairs={{0,4},{4,8},{8,12},{12,0},{1,5},{5,9},{9,13},{13,1},{2,6},{6,10},{... | collective-permute-start | bytes 98312 | tf_op jit(solution)/shard_map/while/body/eval_jaxpr/ppermute | solution.py:24
  40.7 5.7 %collective-permute-start.3 = (bf16[128,128]{1,0:T(8,128)(2,1)S(1)}, bf16[128,128]{1,0:T(8,128)(2,1)S(1)}, u32[]{:S(2)}, u32[]{:S(2)}) collective-permute-start(bf16[128,128]{1,0:T(8,128)(2,1)S(1)} %copy.66), channel_id=1, source_target_pairs={{0,4},{4,8},{8,12},{12,0},{1,5},{5,9},{9,13},{13,1},{2,6},{6,10},{... | collective-permute-start | bytes 98312 | tf_op jit(solution)/shard_map/while/body/eval_jaxpr/ppermute | solution.py:24
  52.4 6.5 %collective-permute-start.8 = (bf16[256,1,128]{2,0,1:T(8,128)(2,1)S(1)}, bf16[256,1,128]{2,0,1:T(8,128)(2,1)S(1)}, u32[]{:S(2)}, u32[]{:S(2)}) collective-permute-start(bf16[256,1,128]{2,0,1:T(8,128)(2,1)S(1)} %convert_element_type.173), channel_id=1, source_target_pairs={{0,4},{4,8},{8,12},{12,0},{1,5},{5,9},{9,13},{13,1},{2,6},{6,10},{... | collective-permute-start | bytes 196616 | tf_op jit(solution)/shard_map/while/body/eval_jaxpr/ppermute | solution.py:24
  52.5 7.1 %collective-permute-start.9 = (bf16[256,1,128]{2,0,1:T(8,128)(2,1)S(1)}, bf16[256,1,128]{2,0,1:T(8,128)(2,1)S(1)}, u32[]{:S(2)}, u32[]{:S(2)}) collective-permute-start(bf16[256,1,128]{2,0,1:T(8,128)(2,1)S(1)} %convert_element_type.175), channel_id=1, source_target_pairs={{0,4},{4,8},{8,12},{12,0},{1,5},{5,9},{9,13},{13,1},{2,6},{6,10},{... | collective-permute-start | bytes 196616 | tf_op jit(solution)/shard_map/while/body/eval_jaxpr/ppermute | solution.py:24
  53.7 6.2 %collective-permute-start.4 = (bf16[128,128]{1,0:T(8,128)(2,1)S(1)}, bf16[128,128]{1,0:T(8,128)(2,1)S(1)}, u32[]{:S(2)}, u32[]{:S(2)}) collective-permute-start(bf16[128,128]{1,0:T(8,128)(2,1)S(1)} %copy.95), channel_id=1, source_target_pairs={{0,4},{4,8},{8,12},{12,0},{1,5},{5,9},{9,13},{13,1},{2,6},{6,10},{... | collective-permute-start | bytes 98312 | tf_op jit(solution)/shard_map/while/body/eval_jaxpr/ppermute | solution.py:24
  55.3 5.7 %collective-permute-start.5 = (bf16[128,128]{1,0:T(8,128)(2,1)S(1)}, bf16[128,128]{1,0:T(8,128)(2,1)S(1)}, u32[]{:S(2)}, u32[]{:S(2)}) collective-permute-start(bf16[128,128]{1,0:T(8,128)(2,1)S(1)} %copy.96), channel_id=1, source_target_pairs={{0,4},{4,8},{8,12},{12,0},{1,5},{5,9},{9,13},{13,1},{2,6},{6,10},{... | collective-permute-start | bytes 98312 | tf_op jit(solution)/shard_map/while/body/eval_jaxpr/ppermute | solution.py:24
  57.5 5.7 %collective-permute-start.6 = (bf16[128,128]{1,0:T(8,128)(2,1)S(1)}, bf16[128,128]{1,0:T(8,128)(2,1)S(1)}, u32[]{:S(2)}, u32[]{:S(2)}) collective-permute-start(bf16[128,128]{1,0:T(8,128)(2,1)S(1)} %copy.97), channel_id=1, source_target_pairs={{0,4},{4,8},{8,12},{12,0},{1,5},{5,9},{9,13},{13,1},{2,6},{6,10},{... | collective-permute-start | bytes 98312 | tf_op jit(solution)/shard_map/while/body/eval_jaxpr/ppermute | solution.py:24
  58.9 5.7 %collective-permute-start.7 = (bf16[128,128]{1,0:T(8,128)(2,1)S(1)}, bf16[128,128]{1,0:T(8,128)(2,1)S(1)}, u32[]{:S(2)}, u32[]{:S(2)}) collective-permute-start(bf16[128,128]{1,0:T(8,128)(2,1)S(1)} %copy.98), channel_id=1, source_target_pairs={{0,4},{4,8},{8,12},{12,0},{1,5},{5,9},{9,13},{13,1},{2,6},{6,10},{... | collective-permute-start | bytes 98312 | tf_op jit(solution)/shard_map/while/body/eval_jaxpr/ppermute | solution.py:24
  69.4 6.1 %collective-permute-start.8 = (bf16[256,1,128]{2,0,1:T(8,128)(2,1)S(1)}, bf16[256,1,128]{2,0,1:T(8,128)(2,1)S(1)}, u32[]{:S(2)}, u32[]{:S(2)}) collective-permute-start(bf16[256,1,128]{2,0,1:T(8,128)(2,1)S(1)} %convert_element_type.173), channel_id=1, source_target_pairs={{0,4},{4,8},{8,12},{12,0},{1,5},{5,9},{9,13},{13,1},{2,6},{6,10},{... | collective-permute-start | bytes 196616 | tf_op jit(solution)/shard_map/while/body/eval_jaxpr/ppermute | solution.py:24
  69.5 6.7 %collective-permute-start.9 = (bf16[256,1,128]{2,0,1:T(8,128)(2,1)S(1)}, bf16[256,1,128]{2,0,1:T(8,128)(2,1)S(1)}, u32[]{:S(2)}, u32[]{:S(2)}) collective-permute-start(bf16[256,1,128]{2,0,1:T(8,128)(2,1)S(1)} %convert_element_type.175), channel_id=1, source_target_pairs={{0,4},{4,8},{8,12},{12,0},{1,5},{5,9},{9,13},{13,1},{2,6},{6,10},{... | collective-permute-start | bytes 196616 | tf_op jit(solution)/shard_map/while/body/eval_jaxpr/ppermute | solution.py:24
  69.6 7.0 %collective-permute-start.4 = (bf16[128,128]{1,0:T(8,128)(2,1)S(1)}, bf16[128,128]{1,0:T(8,128)(2,1)S(1)}, u32[]{:S(2)}, u32[]{:S(2)}) collective-permute-start(bf16[128,128]{1,0:T(8,128)(2,1)S(1)} %copy.95), channel_id=1, source_target_pairs={{0,4},{4,8},{8,12},{12,0},{1,5},{5,9},{9,13},{13,1},{2,6},{6,10},{... | collective-permute-start | bytes 98312 | tf_op jit(solution)/shard_map/while/body/eval_jaxpr/ppermute | solution.py:24
  71.3 5.7 %collective-permute-start.5 = (bf16[128,128]{1,0:T(8,128)(2,1)S(1)}, bf16[128,128]{1,0:T(8,128)(2,1)S(1)}, u32[]{:S(2)}, u32[]{:S(2)}) collective-permute-start(bf16[128,128]{1,0:T(8,128)(2,1)S(1)} %copy.96), channel_id=1, source_target_pairs={{0,4},{4,8},{8,12},{12,0},{1,5},{5,9},{9,13},{13,1},{2,6},{6,10},{... | collective-permute-start | bytes 98312 | tf_op jit(solution)/shard_map/while/body/eval_jaxpr/ppermute | solution.py:24
  74.5 5.7 %collective-permute-start.6 = (bf16[128,128]{1,0:T(8,128)(2,1)S(1)}, bf16[128,128]{1,0:T(8,128)(2,1)S(1)}, u32[]{:S(2)}, u32[]{:S(2)}) collective-permute-start(bf16[128,128]{1,0:T(8,128)(2,1)S(1)} %copy.97), channel_id=1, source_target_pairs={{0,4},{4,8},{8,12},{12,0},{1,5},{5,9},{9,13},{13,1},{2,6},{6,10},{... | collective-permute-start | bytes 98312 | tf_op jit(solution)/shard_map/while/body/eval_jaxpr/ppermute | solution.py:24
  75.5 5.7 %collective-permute-start.7 = (bf16[128,128]{1,0:T(8,128)(2,1)S(1)}, bf16[128,128]{1,0:T(8,128)(2,1)S(1)}, u32[]{:S(2)}, u32[]{:S(2)}) collective-permute-start(bf16[128,128]{1,0:T(8,128)(2,1)S(1)} %copy.98), channel_id=1, source_target_pairs={{0,4},{4,8},{8,12},{12,0},{1,5},{5,9},{9,13},{13,1},{2,6},{6,10},{... | collective-permute-start | bytes 98312 | tf_op jit(solution)/shard_map/while/body/eval_jaxpr/ppermute | solution.py:24
  86.1 6.1 %collective-permute-start.8 = (bf16[256,1,128]{2,0,1:T(8,128)(2,1)S(1)}, bf16[256,1,128]{2,0,1:T(8,128)(2,1)S(1)}, u32[]{:S(2)}, u32[]{:S(2)}) collective-permute-start(bf16[256,1,128]{2,0,1:T(8,128)(2,1)S(1)} %convert_element_type.173), channel_id=1, source_target_pairs={{0,4},{4,8},{8,12},{12,0},{1,5},{5,9},{9,13},{13,1},{2,6},{6,10},{... | collective-permute-start | bytes 196616 | tf_op jit(solution)/shard_map/while/body/eval_jaxpr/ppermute | solution.py:24
  86.2 6.7 %collective-permute-start.9 = (bf16[256,1,128]{2,0,1:T(8,128)(2,1)S(1)}, bf16[256,1,128]{2,0,1:T(8,128)(2,1)S(1)}, u32[]{:S(2)}, u32[]{:S(2)}) collective-permute-start(bf16[256,1,128]{2,0,1:T(8,128)(2,1)S(1)} %convert_element_type.175), channel_id=1, source_target_pairs={{0,4},{4,8},{8,12},{12,0},{1,5},{5,9},{9,13},{13,1},{2,6},{6,10},{... | collective-permute-start | bytes 196616 | tf_op jit(solution)/shard_map/while/body/eval_jaxpr/ppermute | solution.py:24
  86.3 7.2 %collective-permute-start.4 = (bf16[128,128]{1,0:T(8,128)(2,1)S(1)}, bf16[128,128]{1,0:T(8,128)(2,1)S(1)}, u32[]{:S(2)}, u32[]{:S(2)}) collective-permute-start(bf16[128,128]{1,0:T(8,128)(2,1)S(1)} %copy.95), channel_id=1, source_target_pairs={{0,4},{4,8},{8,12},{12,0},{1,5},{5,9},{9,13},{13,1},{2,6},{6,10},{... | collective-permute-start | bytes 98312 | tf_op jit(solution)/shard_map/while/body/eval_jaxpr/ppermute | solution.py:24
  88.7 6.1 %collective-permute-start.5 = (bf16[128,128]{1,0:T(8,128)(2,1)S(1)}, bf16[128,128]{1,0:T(8,128)(2,1)S(1)}, u32[]{:S(2)}, u32[]{:S(2)}) collective-permute-start(bf16[128,128]{1,0:T(8,128)(2,1)S(1)} %copy.96), channel_id=1, source_target_pairs={{0,4},{4,8},{8,12},{12,0},{1,5},{5,9},{9,13},{13,1},{2,6},{6,10},{... | collective-permute-start | bytes 98312 | tf_op jit(solution)/shard_map/while/body/eval_jaxpr/ppermute | solution.py:24
  91.2 5.7 %collective-permute-start.6 = (bf16[128,128]{1,0:T(8,128)(2,1)S(1)}, bf16[128,128]{1,0:T(8,128)(2,1)S(1)}, u32[]{:S(2)}, u32[]{:S(2)}) collective-permute-start(bf16[128,128]{1,0:T(8,128)(2,1)S(1)} %copy.97), channel_id=1, source_target_pairs={{0,4},{4,8},{8,12},{12,0},{1,5},{5,9},{9,13},{13,1},{2,6},{6,10},{... | collective-permute-start | bytes 98312 | tf_op jit(solution)/shard_map/while/body/eval_jaxpr/ppermute | solution.py:24
  92.2 5.7 %collective-permute-start.7 = (bf16[128,128]{1,0:T(8,128)(2,1)S(1)}, bf16[128,128]{1,0:T(8,128)(2,1)S(1)}, u32[]{:S(2)}, u32[]{:S(2)}) collective-permute-start(bf16[128,128]{1,0:T(8,128)(2,1)S(1)} %copy.98), channel_id=1, source_target_pairs={{0,4},{4,8},{8,12},{12,0},{1,5},{5,9},{9,13},{13,1},{2,6},{6,10},{... | collective-permute-start | bytes 98312 | tf_op jit(solution)/shard_map/while/body/eval_jaxpr/ppermute | solution.py:24
  99.2 6.1 %collective-permute-start.11 = (bf16[256,1,128]{2,0,1:T(8,128)(2,1)S(1)}, bf16[256,1,128]{2,0,1:T(8,128)(2,1)S(1)}, u32[]{:S(2)}, u32[]{:S(2)}) collective-permute-start(bf16[256,1,128]{2,0,1:T(8,128)(2,1)S(1)} %convert_element_type.122), channel_id=1, source_target_pairs={{0,4},{4,8},{8,12},{12,0},{1,5},{5,9},{9,13},{13,1},{2,6},{6,10},{... | collective-permute-start | bytes 196616 | tf_op jit(solution)/shard_map/ppermute | solution.py:24
  99.3 0.8 copy-start.10
  99.3 6.7 %collective-permute-start.10 = (bf16[256,1,128]{2,0,1:T(8,128)(2,1)S(1)}, bf16[256,1,128]{2,0,1:T(8,128)(2,1)S(1)}, u32[]{:S(2)}, u32[]{:S(2)}) collective-permute-start(bf16[256,1,128]{2,0,1:T(8,128)(2,1)S(1)} %convert_element_type.119), channel_id=1, source_target_pairs={{0,4},{4,8},{8,12},{12,0},{1,5},{5,9},{9,13},{13,1},{2,6},{6,10},{... | collective-permute-start | bytes 196616 | tf_op jit(solution)/shard_map/ppermute | solution.py:24
  105.3 0.7 copy-start.6
  106.0 0.6 copy-start.7
  106.7 90.4 %all-reduce.5.cloned.1.call-start = ((), (), s32[]{:S(2)}) async-start(), calls=%async_computation | async-start | bytes 131072 | tf_op jit(solution)/shard_map/psum | solution.py:217
  137.8 0.9 copy-start.11
  138.6 25.1 %copy-start.1 = (bf16[256,128]{1,0:T(8,128)(2,1)}, bf16[256,128]{1,0:T(8,128)(2,1)S(1)}, u32[]{:S(2)}) copy-start(bf16[256,128]{1,0:T(8,128)(2,1)S(1)} %fusion.71) | copy-start | bytes 196612
  163.8 33.3 %copy-start.5 = (bf16[256,128]{1,0:T(8,128)(2,1)S(1)}, bf16[256,128]{1,0:T(8,128)(2,1)}, u32[]{:S(2)}) copy-start(bf16[256,128]{1,0:T(8,128)(2,1)} %get-tuple-element.1579) | copy-start | bytes 196612
  197.1 0.9 copy-start.8
Sparse Core Ops, SparseCore 0:
  106.8 30.8 all-reduce.6
  163.9 33.1 all-reduce.4
